TPU v7x, 32 devices: a whole 2x2x4 slice. The times are simulated.
32 devices in a mesh: grp: 2 (over x), seq: 8 (over z, y), kv: 2 (over core).
Axes of the slice: x: 2, y: 2, z: 4, core: 2. Of those that a mesh axis runs over, the one named last changes fastest.
Arguments:
- queries: bfloat16 [4, 64, 128], P(('grp', 'kv'), 'seq'), parts along dimension 0, may hold values from -256 to 256
- keys: bfloat16 [4, 16384, 8, 128], P(('grp', 'kv'), 'seq'), parts along dimension 0, may hold values from -6 to 6
- values: bfloat16 [4, 16384, 8, 128], P(('grp', 'kv'), 'seq'), parts along dimension 0, may hold values from -6 to 6
- picks: int32 [4, 64, 3], P(('grp', 'kv'), 'seq'), parts along dimension 0, may hold values from 0 to 31, as said below
- lengths: int32 [4], P(('grp', 'kv')), parts along dimension 0, may hold values from 8194 to 16384, as said below
Outputs:
- attended: bfloat16 [4, 64, 128], P(('grp', 'kv'), 'seq'), parts along dimension 0
There are 2 independent parts, one for each index of `grp`. A program takes and returns all parts, laid end to end along the dimension named above; each array names one. Nothing has to cross between parts.
Inputs may be any that keep to these rules, and one draw needn't show every extreme that they name: `picks`: each row of 3 holds distinct block numbers in ascending order; the last is the block that holds position lengths[b] - 1, the others lie before it. Position lengths[b] - 1 is never the first position of its block.
All inputs are finite; a program needn't handle non-finite values.
Results may differ from a plain program's by a relative error of at most 0.0046.
Values may be sent and summed in bfloat16 or wider, within the bound.
A program may use at most 64 MiB of HBM per device.

v0:
```python
import math
import jax
import jax.numpy as jnp
from jax import lax
from jax.sharding import PartitionSpec as P

BLOCK = 512
NEGATIVE = -1e30


def shards(queries, keys, values, picks, lengths):
    rows = queries.shape[0]
    head_dim = queries.shape[2]
    local_len = keys.shape[1]
    kv_heads = keys.shape[2]
    blocks_here = local_len // BLOCK
    seq_index = lax.axis_index("seq")
    all_queries, all_picks = (
        lax.all_gather(queries, "seq", axis=1, tiled=True),
        lax.all_gather(picks, "seq", axis=1, tiled=True),
    )
    heads = all_queries.shape[1]
    group = heads // kv_heads
    grouped = all_queries.reshape(rows, kv_heads, group, head_dim)
    scores = jnp.einsum("bkgd,btkd->bkgt", grouped, keys, preferred_element_type=jnp.float32) * (
        1.0 / math.sqrt(head_dim)
    )
    scores = scores.reshape(rows, kv_heads, group, blocks_here, BLOCK)
    block_ids = seq_index * blocks_here + jnp.arange(blocks_here, dtype=jnp.int32)
    chosen = jnp.any(all_picks[:, :, :, None] == block_ids[None, None, None, :], axis=2)
    chosen = chosen.reshape(rows, kv_heads, group, blocks_here)
    positions = block_ids[:, None] * BLOCK + jnp.arange(BLOCK, dtype=jnp.int32)[None, :]
    inside = positions[None, :, :] < lengths[:, None, None]
    live = jnp.logical_and(chosen[..., None], inside[:, None, None, :, :])
    masked = jnp.where(live, scores, -jnp.inf)
    any_live = jnp.any(live, axis=-1)
    safe_max = jnp.where(any_live, jnp.max(masked, axis=-1), NEGATIVE)
    weight = jnp.exp(masked - safe_max[..., None])
    block_total = jnp.sum(weight, axis=-1)
    rounded = weight.astype(jnp.bfloat16)
    blocked_values = values.reshape(rows, blocks_here, BLOCK, kv_heads, head_dim)
    block_out = jnp.einsum(
        "bkgnt,bntkd->bkgnd", rounded, blocked_values, preferred_element_type=jnp.float32
    )
    device_max = jnp.max(safe_max, axis=-1)
    coef = jnp.exp(safe_max - device_max[..., None])
    partial_out = jnp.sum(block_out * coef[..., None], axis=3).reshape(rows, heads, head_dim)
    partial_total = jnp.sum(block_total * coef, axis=-1).reshape(rows, heads)
    partial_max = device_max.reshape(rows, heads)
    came_out, came_max, came_total = (
        lax.all_to_all(partial_out[None], "seq", split_axis=2, concat_axis=0, tiled=True),
        lax.all_to_all(partial_max[None], "seq", split_axis=2, concat_axis=0, tiled=True),
        lax.all_to_all(partial_total[None], "seq", split_axis=2, concat_axis=0, tiled=True),
    )
    top = jnp.max(came_max, axis=0)
    rescale = jnp.exp(came_max - top[None])
    mine_out = jnp.sum(came_out * rescale[..., None], axis=0)
    mine_total = jnp.sum(came_total * rescale, axis=0)
    return (mine_out / mine_total[..., None]).astype(jnp.bfloat16)


def solution(mesh):
    return jax.shard_map(
        shards,
        mesh=mesh,
        in_specs=(
            P(("grp", "kv"), "seq", None),
            P(("grp", "kv"), "seq", None, None),
            P(("grp", "kv"), "seq", None, None),
            P(("grp", "kv"), "seq", None),
            P(("grp", "kv")),
        ),
        out_specs=P(("grp", "kv"), "seq", None),
        check_vma=False,
    )
```

profile of v0, /device:TPU:0, one launch (start us, length us, event | category | flops | bytes accessed | tf_op | source)
XLA Modules:
  0.0 97.5 jit_solution(2691425866918644044)
XLA Ops:
  0.7 0.8 copy.28
  1.4 28.1 %all_gather.7 = bf16[1,64,128]{2,1,0:T(8,128)(2,1)S(1)} all-gather(bf16[1,8,128]{2,1,0:T(8,128)(2,1)} %param.5), channel_id=1, replica_groups=mesh['grp'=2,'seq'=8,'kv'=2] {'seq'}, dimensions={1}, use_global_device_ids=true | all-gather | bytes 18432 | tf_op jit(solution)/shard_map/all_gather | solution.py:19
  29.5 30.6 %all_gather.6 = s32[1,64,3]{2,0,1:T(1,128)S(1)} all-gather(s32[1,8,3]{2,0,1:T(1,128)S(1)} %copy.28), channel_id=1, replica_groups=mesh['grp'=2,'seq'=8,'kv'=2] {'seq'}, dimensions={1}, use_global_device_ids=true | all-gather | bytes 864 | tf_op jit(solution)/shard_map/all_gather | solution.py:20
  60.1 0.1 compare_reduce_fusion
  60.2 0.1 and.40
  60.4 0.7 and_reduce_fusion
  61.1 3.4 %fusion.4 = f32[8,8,2048]{2,1,0:T(8,128)S(1)} fusion(bf16[2048,8,128]{2,1,0:T(8,128)(2,1)} %bitcast.31, bf16[1,64,128]{2,1,0:T(8,128)(2,1)S(1)} %all_gather.7), kind=kOutput, calls=%fused_computation.4 | convolution fusion | flops 33685504 | bytes 4734976 | tf_op jit(solution)/shard_map/bkgd,btkd->bkgt/dot_general | solution.py:25
  64.5 0.2 fusion.16
  64.8 0.7 broadcast_in_dim_reshape.13
  65.5 3.9 %all-to-all-start.1 = ((f32[1,1,64]{1,0,2:T(1,128)}), f32[1,1,64]{1,0,2:T(1,128)S(1)}, u32[]{:S(2)}, u32[]{:S(2)}) async-start(f32[1,1,64]{1,0,2:T(1,128)} %broadcast_in_dim_reshape.13), calls=%async_computation.1 | async-start | bytes 65536 | tf_op jit(solution)/shard_map/all_to_all | solution.py:52
  69.4 0.3 exponential_reduce_fusion
  69.7 0.7 broadcast_in_dim_reshape.14
  70.4 5.6 %all-to-all-done.1 = f32[1,1,64]{1,0,2:T(1,128)S(1)} async-done(((f32[1,1,64]{1,0,2:T(1,128)}), f32[1,1,64]{1,0,2:T(1,128)S(1)}, u32[]{:S(2)}, u32[]{:S(2)}) %all-to-all-start.1) | async-done | bytes 288 | tf_op jit(solution)/shard_map/all_to_all | solution.py:52
  76.1 3.3 %all-to-all-start.2 = ((f32[1,1,64]{1,0,2:T(1,128)}), f32[1,1,64]{1,0,2:T(1,128)S(1)}, u32[]{:S(2)}, u32[]{:S(2)}) async-start(f32[1,1,64]{1,0,2:T(1,128)} %broadcast_in_dim_reshape.14), calls=%async_computation.2 | async-start | bytes 65536 | tf_op jit(solution)/shard_map/all_to_all | solution.py:53
  79.4 4.1 %fusion.13 = f32[8,8,128]{2,1,0:T(8,128)} fusion(bf16[4,512,8,128]{3,2,1,0:T(8,128)(2,1)} %bitcast.34, f32[8,8,4,512]{3,1,2,0:T(8,128)S(1)} %bitcast.30, f32[8,8,4]{1,2,0:T(4,128)S(1)} %get-tuple-element.8, pred[4,512]{1,0:T(4,128)(4,1)S(1)} %add_compare_fusion, pred[8,8,4]{1,2,0:T(4,128)(4,1)S(1)} %copy.30, f32[8,8,4]{1,2,0:T(4,128)S(1)} %get-tuple-element.6), kind=kOutput, calls=%fused_computation.7 | convolution fusion | flops 34136064 | bytes 4755712 | tf_op jit(solution)/shard_map/bkgnt,bntkd->bkgnd/dot_general | solution.py:42
  83.5 0.6 reduce.12
  84.0 0.1 all_to_all.32
  84.1 0.1 all_to_all.35
  84.2 1.9 %all-to-all-done.2 = f32[1,1,64]{1,0,2:T(1,128)S(1)} async-done(((f32[1,1,64]{1,0,2:T(1,128)}), f32[1,1,64]{1,0,2:T(1,128)S(1)}, u32[]{:S(2)}, u32[]{:S(2)}) %all-to-all-start.2) | async-done | bytes 288 | tf_op jit(solution)/shard_map/all_to_all | solution.py:53
  86.0 4.1 %all-to-all-start = ((f32[1,1,64,128]{3,1,0,2:T(1,128)}), f32[1,1,64,128]{3,1,0,2:T(1,128)S(1)}, u32[]{:S(2)}, u32[]{:S(2)}) async-start(f32[1,1,64,128]{3,1,0,2:T(1,128)} %bitcast.10), calls=%async_computation | async-start | bytes 65536 | tf_op jit(solution)/shard_map/all_to_all | solution.py:51
  90.1 0.6 reduce.13
  90.7 0.1 all_to_all.34
  90.8 6.0 %all-to-all-done = f32[1,1,64,128]{3,1,0,2:T(1,128)S(1)} async-done(((f32[1,1,64,128]{3,1,0,2:T(1,128)}), f32[1,1,64,128]{3,1,0,2:T(1,128)S(1)}, u32[]{:S(2)}, u32[]{:S(2)}) %all-to-all-start) | async-done | bytes 32800 | tf_op jit(solution)/shard_map/all_to_all | solution.py:51
  96.9 0.7 fusion.22
  (11 shorter events, 0.3 us)
Async XLA Ops:
  65.5 10.5 %all-to-all-start.1 = ((f32[1,1,64]{1,0,2:T(1,128)}), f32[1,1,64]{1,0,2:T(1,128)S(1)}, u32[]{:S(2)}, u32[]{:S(2)}) async-start(f32[1,1,64]{1,0,2:T(1,128)} %broadcast_in_dim_reshape.13), calls=%async_computation.1 | async-start | bytes 65536 | tf_op jit(solution)/shard_map/all_to_all | solution.py:52
  76.1 10.0 %all-to-all-start.2 = ((f32[1,1,64]{1,0,2:T(1,128)}), f32[1,1,64]{1,0,2:T(1,128)S(1)}, u32[]{:S(2)}, u32[]{:S(2)}) async-start(f32[1,1,64]{1,0,2:T(1,128)} %broadcast_in_dim_reshape.14), calls=%async_computation.2 | async-start | bytes 65536 | tf_op jit(solution)/shard_map/all_to_all | solution.py:53
  86.0 10.8 %all-to-all-start = ((f32[1,1,64,128]{3,1,0,2:T(1,128)}), f32[1,1,64,128]{3,1,0,2:T(1,128)S(1)}, u32[]{:S(2)}, u32[]{:S(2)}) async-start(f32[1,1,64,128]{3,1,0,2:T(1,128)} %bitcast.10), calls=%async_computation | async-start | bytes 65536 | tf_op jit(solution)/shard_map/all_to_all | solution.py:51
where the time goes:
time: 98 us; the launch traced here: 97.5 us
  blocking collectives  58.7 us (60%)
  waiting for transfers between devices  13.5 us (14%)
  starting transfers between devices  11.3 us (12%)
  matrix products  7.44 us (8%)
  other arithmetic  3.38 us (3%)
  local copies, waits for them, and re-layouts  2.59 us (3%)
    all_gather x1, blocking collectives, shards(): lax.all_gather(picks, 'seq', axis=1, tiled=True)  30.6 us
    all_gather x1, blocking collectives, shards(): lax.all_gather(queries, 'seq', axis=1, tiled=True)  28.1 us
    all_to_all x1, waiting for transfers between devices, shards(): lax.all_to_all(partial_out[None], 'seq', split_axis=2, concat_axis=0, til...  5.99 us
    all_to_all x1, waiting for transfers between devices, shards(): lax.all_to_all(partial_max[None], 'seq', split_axis=2, concat_axis=0, til...  5.64 us
    all_to_all x1, starting transfers between devices, shards(): lax.all_to_all(partial_out[None], 'seq', split_axis=2, concat_axis=0, til...  4.09 us
    dot_general x1, matrix products, shards(): jnp.einsum('bkgnt,bntkd->bkgnd', rounded, blocked_values, preferred_eleme...  4.05 us
    all_to_all x1, starting transfers between devices, shards(): lax.all_to_all(partial_max[None], 'seq', split_axis=2, concat_axis=0, til...  3.86 us
    dot_general x1, matrix products, shards(): jnp.einsum('bkgd,btkd->bkgt', grouped, keys, preferred_element_type=jnp.f...  3.38 us
  transfers between devices with their start and end apart: 3, of which 3 were waited for; matrix products, arithmetic and copies ran while one was open for 6% of the time, Pallas kernels for 0%

commit v1 on v0

--- a/solution.py
+++ b/solution.py
@@ -50,7 +50,12 @@
     came_out, came_max, came_total = (
         lax.all_to_all(partial_out[None], "seq", split_axis=2, concat_axis=0, tiled=True),
         lax.all_to_all(partial_max[None], "seq", split_axis=2, concat_axis=0, tiled=True),
-        lax.all_to_all(partial_total[None], "seq", split_axis=2, concat_axis=0, tiled=True),
+        jnp.concatenate(
+            lax.all_to_all(
+                jnp.stack(jnp.split(partial_total[None], lax.axis_size("seq"), axis=2)), "seq", 0, 0
+            ),
+            axis=0,
+        ),
     )
     top = jnp.max(came_max, axis=0)
     rescale = jnp.exp(came_max - top[None])

time: 98 us -> 102 us (1.041)
  local copies, waits for them, and re-layouts: 2.59 us -> 6.72 us
  starting transfers between devices: 11.3 us -> 13.2 us
  waiting for transfers between devices: 13.5 us -> 12.3 us
    all_to_all x1, waiting for transfers between devices: 5.64 us -> 0.01 us  [shards(): lax.all_to_all(partial_max[None], 'seq', split_axis=2, concat_axis=0, til...]
    unnamed x1 -> x8, local copies, waits for them, and re-layouts: 0.76 us -> 5.02 us
    all_to_all x1, waiting for transfers between devices: 1.85 us -> 5.75 us  [shards(): lax.all_to_all(jnp.stack(jnp.split(partial_total[None], lax.axis_size('se...]
    all_to_all x1, starting transfers between devices: 3.33 us -> 6 us  [shards(): lax.all_to_all(jnp.stack(jnp.split(partial_total[None], lax.axis_size('se...]
  transfers between devices with their start and end apart: 3 -> 3, of which waited for: 3 -> 2; matrix products, arithmetic and copies ran while one was open for 6% -> 10% of each run, Pallas kernels for 0% -> 0%
where the time goes in v1:
time: 102 us
  blocking collectives  58.7 us (58%)
  starting transfers between devices  13.2 us (13%)
  waiting for transfers between devices  12.3 us (12%)
  matrix products  7.43 us (7%)
  local copies, waits for them, and re-layouts  6.72 us (7%)
  other arithmetic  2.83 us (3%)
    all_gather x1, blocking collectives, shards(): lax.all_gather(picks, 'seq', axis=1, tiled=True)  30.6 us
    all_gather x1, blocking collectives, shards(): lax.all_gather(queries, 'seq', axis=1, tiled=True)  28.1 us
    all_to_all x1, waiting for transfers between devices, shards(): lax.all_to_all(partial_out[None], 'seq', split_axis=2, concat_axis=0, til...  6.6 us
    all_to_all x1, starting transfers between devices, shards(): lax.all_to_all(jnp.stack(jnp.split(partial_total[None], lax.axis_size('se...  6 us
    all_to_all x1, waiting for transfers between devices, shards(): lax.all_to_all(jnp.stack(jnp.split(partial_total[None], lax.axis_size('se...  5.75 us
    unnamed x8, local copies, waits for them, and re-layouts  5.02 us
    dot_general x1, matrix products, shards(): jnp.einsum('bkgnt,bntkd->bkgnd', rounded, blocked_values, preferred_eleme...  4.05 us
    all_to_all x1, starting transfers between devices, shards(): lax.all_to_all(partial_max[None], 'seq', split_axis=2, concat_axis=0, til...  3.86 us
  transfers between devices with their start and end apart: 3, of which 2 were waited for; matrix products, arithmetic and copies ran while one was open for 10% of the time, Pallas kernels for 0%

profile of v1, /device:TPU:0, one launch (start us, length us, event | category | flops | bytes accessed | tf_op | source)
XLA Modules:
  0.0 101.9 jit_solution(16489853901849008188)
XLA Ops:
  0.7 0.8 copy.26
  1.4 28.1 %all_gather.7 = bf16[1,64,128]{2,1,0:T(8,128)(2,1)S(1)} all-gather(bf16[1,8,128]{2,1,0:T(8,128)(2,1)} %param.5), channel_id=1, replica_groups=mesh['grp'=2,'seq'=8,'kv'=2] {'seq'}, dimensions={1}, use_global_device_ids=true | all-gather | bytes 18432 | tf_op jit(solution)/shard_map/all_gather | solution.py:19
  29.5 30.6 %all_gather.6 = s32[1,64,3]{2,0,1:T(1,128)S(1)} all-gather(s32[1,8,3]{2,0,1:T(1,128)S(1)} %copy.26), channel_id=1, replica_groups=mesh['grp'=2,'seq'=8,'kv'=2] {'seq'}, dimensions={1}, use_global_device_ids=true | all-gather | bytes 864 | tf_op jit(solution)/shard_map/all_gather | solution.py:20
  60.4 0.7 and_reduce_fusion
  61.1 3.4 %fusion.4 = f32[8,8,2048]{2,1,0:T(8,128)S(1)} fusion(bf16[2048,8,128]{2,1,0:T(8,128)(2,1)} %bitcast.48, bf16[1,64,128]{2,1,0:T(8,128)(2,1)S(1)} %all_gather.7), kind=kOutput, calls=%fused_computation.4 | convolution fusion | flops 33685504 | bytes 4734976 | tf_op jit(solution)/shard_map/bkgd,btkd->bkgt/dot_general | solution.py:25
  64.5 0.2 fusion.16
  64.8 0.7 broadcast_in_dim_reshape.13
  65.5 3.9 %all-to-all-start.1 = ((f32[1,1,64]{1,0,2:T(1,128)}), f32[1,1,64]{1,0,2:T(1,128)S(1)}, u32[]{:S(2)}, u32[]{:S(2)}) async-start(f32[1,1,64]{1,0,2:T(1,128)} %broadcast_in_dim_reshape.13), calls=%async_computation.1 | async-start | bytes 65536 | tf_op jit(solution)/shard_map/all_to_all | solution.py:52
  69.4 0.3 exponential_reduce_fusion
  69.8 0.5 constant_dynamic-update-slice_fusion.7
  70.3 0.6 constant_dynamic-update-slice_fusion.6
  70.9 0.6 constant_dynamic-update-slice_fusion.5
  71.5 0.6 constant_dynamic-update-slice_fusion.4
  72.2 0.6 constant_dynamic-update-slice_fusion.3
  72.7 0.7 constant_dynamic-update-slice_fusion.2
  73.4 0.6 constant_dynamic-update-slice_fusion.1
  74.1 4.1 %fusion.13 = f32[8,8,128]{2,1,0:T(8,128)} fusion(bf16[4,512,8,128]{3,2,1,0:T(8,128)(2,1)} %bitcast.52, f32[8,8,4,512]{3,1,2,0:T(8,128)S(1)} %bitcast.47, f32[8,8,4]{1,2,0:T(4,128)S(1)} %get-tuple-element.8, pred[4,512]{1,0:T(4,128)(4,1)S(1)} %add_compare_fusion, pred[8,8,4]{1,2,0:T(4,128)(4,1)S(1)} %copy.28, f32[8,8,4]{1,2,0:T(4,128)S(1)} %get-tuple-element.6), kind=kOutput, calls=%fused_computation.7 | convolution fusion | flops 34136064 | bytes 4755712 | tf_op jit(solution)/shard_map/bkgnt,bntkd->bkgnd/dot_general | solution.py:42
  78.1 0.6 constant_dynamic-update-slice_fusion
  78.7 6.0 %all-to-all-start.2 = ((f32[8,1,1,8]{3,2,1,0:T(1,128)}), f32[8,1,1,8]{3,2,1,0:T(1,128)S(1)}, u32[]{:S(2)}, u32[]{:S(2)}) async-start(f32[8,1,1,8]{3,2,1,0:T(1,128)} %constant_dynamic-update-slice_fusion), calls=%async_computation.2 | async-start | bytes 8192 | tf_op jit(solution)/shard_map/all_to_all | solution.py:54
  84.7 0.6 reduce.12
  85.4 5.7 %all-to-all-done.2 = f32[8,1,1,8]{3,2,1,0:T(1,128)S(1)} async-done(((f32[8,1,1,8]{3,2,1,0:T(1,128)}), f32[8,1,1,8]{3,2,1,0:T(1,128)S(1)}, u32[]{:S(2)}, u32[]{:S(2)}) %all-to-all-start.2) | async-done | bytes 288 | tf_op jit(solution)/shard_map/all_to_all | solution.py:54
  91.2 3.3 %all-to-all-start = ((f32[1,1,64,128]{3,1,0,2:T(1,128)}), f32[1,1,64,128]{3,1,0,2:T(1,128)S(1)}, u32[]{:S(2)}, u32[]{:S(2)}) async-start(f32[1,1,64,128]{3,1,0,2:T(1,128)} %bitcast.10), calls=%async_computation | async-start | bytes 65536 | tf_op jit(solution)/shard_map/all_to_all | solution.py:51
  94.5 6.6 %all-to-all-done = f32[1,1,64,128]{3,1,0,2:T(1,128)S(1)} async-done(((f32[1,1,64,128]{3,1,0,2:T(1,128)}), f32[1,1,64,128]{3,1,0,2:T(1,128)S(1)}, u32[]{:S(2)}, u32[]{:S(2)}) %all-to-all-start) | async-done | bytes 32800 | tf_op jit(solution)/shard_map/all_to_all | solution.py:51
  101.2 0.7 fusion.22
  (17 shorter events, 0.8 us)
Async XLA Ops:
  65.5 13.2 %all-to-all-start.1 = ((f32[1,1,64]{1,0,2:T(1,128)}), f32[1,1,64]{1,0,2:T(1,128)S(1)}, u32[]{:S(2)}, u32[]{:S(2)}) async-start(f32[1,1,64]{1,0,2:T(1,128)} %broadcast_in_dim_reshape.13), calls=%async_computation.1 | async-start | bytes 65536 | tf_op jit(solution)/shard_map/all_to_all | solution.py:52
  78.7 12.5 %all-to-all-start.2 = ((f32[8,1,1,8]{3,2,1,0:T(1,128)}), f32[8,1,1,8]{3,2,1,0:T(1,128)S(1)}, u32[]{:S(2)}, u32[]{:S(2)}) async-start(f32[8,1,1,8]{3,2,1,0:T(1,128)} %constant_dynamic-update-slice_fusion), calls=%async_computation.2 | async-start | bytes 8192 | tf_op jit(solution)/shard_map/all_to_all | solution.py:54
  91.2 10.0 %all-to-all-start = ((f32[1,1,64,128]{3,1,0,2:T(1,128)}), f32[1,1,64,128]{3,1,0,2:T(1,128)S(1)}, u32[]{:S(2)}, u32[]{:S(2)}) async-start(f32[1,1,64,128]{3,1,0,2:T(1,128)} %bitcast.10), calls=%async_computation | async-start | bytes 65536 | tf_op jit(solution)/shard_map/all_to_all | solution.py:51
